TPU v7x, 32 devices: a whole 2x2x4 slice. The times are simulated.
32 devices in a mesh: dp: 32 (over z, y, x, core).
Axes of the slice: x: 2, y: 2, z: 4, core: 2. Of those that a mesh axis runs over, the one named last changes fastest.
Arguments:
- grads: float32 [32, 163840], P('dp'), may hold values from -6 to 6
- master: float32 [163840], P('dp')
- moment1: float32 [163840], P('dp'), may hold values from -4 to 4
- moment2: float32 [163840], P('dp'), may hold values from 0.1 to 2
- tensor_rows: int32 [8], replicated, may hold values from 1 to 16, 32 in all
- step_count: int32 [1], replicated, may hold values from 1 to 19
Outputs:
- new_weights: bfloat16 [163840], replicated
- new_master: float32 [163840], P('dp')
- new_moment1: float32 [163840], P('dp')
- new_moment2: float32 [163840], P('dp')
All inputs are finite; a program needn't handle non-finite values.
Results may differ from a plain program's by a relative error of at most 0.001.
Values may be sent and summed in bfloat16 or wider, within the bound.
A program may use at most 64 MiB of HBM per device.

v0:
```python
import functools

import jax
import jax.numpy as jnp
import numpy as np
from jax import lax
from jax.experimental import pallas as pl
from jax.experimental.pallas import tpu as pltpu
from jax.sharding import PartitionSpec as P

LANES = 128
BETA1, BETA2 = 0.9, 0.999
STEP_BITS = 8


def levels(count):
    chips = count // 2
    bits = chips.bit_length() - 1
    plane = 1 << ((bits + 1) // 2)
    return chips // plane, plane


def flipped(value, mask):
    bit = 1
    while bit <= mask:
        if mask & bit:
            value = value + bit * (1 - 2 * (value // bit % 2))
        bit *= 2
    return value


def power(base, step):
    result = jnp.ones(step.shape, jnp.float32)
    for bit in range(STEP_BITS):
        factor = float(np.float32(float(np.float32(base)) ** (2**bit)))
        result = result * jnp.where((step // 2**bit) % 2 == 1, factor, 1.0)
    return result


def kernel(
    count, line, plane,
    grads, master, moment1, moment2, rows_in, step_ref,
    masters, guesses, deltas, ratios, m1_new, m2_new, mine,
    theirs, ours, pair_send, pair_recv, plane_send, plane_recv,
    line_send, line_recv, m1, m2, wsums, usums, rows_ref,
    local_sem, send_sem, recv_sem,
):
    me = lax.axis_index("dp")
    core = me % 2
    xy = me // 2 % plane
    z = me // (2 * plane)
    other = 1 - core
    partner = me + 1 - 2 * core
    far_first = list(range(line - 1, 0, -1))
    diagonal_first = list(range(plane - 1, 0, -1))

    def plane_peer(mask):
        return (z * plane + flipped(xy, mask)) * 2 + core

    def line_peer(mask):
        return (flipped(z, mask) * plane + xy) * 2 + core

    peers = [partner] + [plane_peer(k) for k in range(1, plane)]
    peers += [line_peer(k) for k in range(1, line)]
    barrier = pltpu.get_barrier_semaphore()
    for peer in peers:
        pl.semaphore_signal(barrier, inc=1, device_id=(peer,), device_id_type=pl.DeviceIdType.MESH)

    used = {"local": 0, "remote": 0}
    sent = []

    def local(source, target):
        copy = pltpu.make_async_copy(source, target, local_sem.at[used["local"]])
        used["local"] += 1
        copy.start()
        return copy

    def remote(source, target, peer):
        slot = used["remote"]
        used["remote"] += 1
        copy = pltpu.make_async_remote_copy(
            src_ref=source, dst_ref=target,
            send_sem=send_sem.at[slot], recv_sem=recv_sem.at[slot],
            device_id=(peer,), device_id_type=pl.DeviceIdType.MESH,
        )
        copy.start()
        sent.append(copy)
        return copy

    def share(ref, peer):
        return remote(ref, ref, peer)

    layers = far_first + [0]
    their_loads = [local(grads.at[flipped(z, k), :, other], theirs.at[k]) for k in layers]
    master_load = local(master, masters.at[core, xy, z])
    our_loads = [local(grads.at[flipped(z, k), :, core], ours.at[k]) for k in layers]
    moment_loads = [local(moment1, m1), local(moment2, m2)]
    rows_load = local(rows_in, rows_ref)
    step = jnp.full((8, LANES), step_ref[0], jnp.int32)
    first_scale = 1.0 - power(BETA1, step)
    second_scale = 1.0 - power(BETA2, step)

    def update_of(first, second, weight):
        return (first / first_scale) / (jnp.sqrt(second / second_scale) + 1e-06) + 0.1 * weight


    for k, load in zip(layers, their_loads):
        load.wait()
        pair_send[k] = theirs[k].astype(jnp.bfloat16)
    master_load.wait()
    pl.semaphore_wait(barrier, len(peers))

    pair_copies = [remote(pair_send.at[k], pair_recv.at[k], partner) for k in layers]
    early = (masters, guesses)
    early_line = {k: [share(masters.at[core, xy, z], line_peer(k))] for k in far_first}
    for copy in moment_loads:
        copy.wait()
    guess = update_of(0.9 * m1[...], 0.999 * m2[...], masters[core, xy, z]).astype(jnp.bfloat16)
    guesses[core, xy, z] = guess
    early_plane = {p: [] for p in diagonal_first}

    def early_spread(at_z):
        for p in diagonal_first:
            for table in early:
                early_plane[p].append(share(table.at[core, xy, at_z], plane_peer(p)))

    for k in far_first:
        early_line[k].append(share(guesses.at[core, xy, z], line_peer(k)))

    plane_copies = {}
    for k, load, copy in zip(layers, our_loads, pair_copies):
        load.wait()
        copy.wait_recv()
        for p in diagonal_first:
            at = flipped(xy, p)
            chip = ours[k, at] + pair_recv[k, at].astype(jnp.float32)
            plane_send[k, p - 1] = chip.astype(jnp.bfloat16)
            plane_copies[k, p] = remote(plane_send.at[k, p - 1], plane_recv.at[k, p - 1], plane_peer(p))

    early_spread(z)

    def plane_sum(k):
        total = ours[k, xy] + pair_recv[k, xy].astype(jnp.float32)
        for p in diagonal_first:
            plane_copies[k, p].wait_recv()
            total = total + plane_recv[k, p - 1].astype(jnp.float32)
        return total

    line_copies = []
    for k, near in zip(far_first, reversed(far_first)):
        line_send[k - 1] = plane_sum(k).astype(jnp.bfloat16)
        line_copies.append((k, remote(line_send.at[k - 1], line_recv.at[k - 1], line_peer(k))))

        for copy in early_line[near]:
            copy.wait_recv()
        early_spread(flipped(z, near))
    early_pair = {0: [share(table.at[core, xy], partner) for table in early]}

    grad = plane_sum(0)
    for k, copy in line_copies:
        copy.wait_recv()
        grad = grad + line_recv[k - 1].astype(jnp.float32)
    grad = grad / jnp.float32(count)
    new_m1 = 0.9 * m1[...] + 0.1 * grad
    new_m2 = 0.999 * m2[...] + 0.001 * grad * grad
    update = update_of(new_m1, new_m2, masters[core, xy, z])
    deltas[core, xy, z] = (update - guess.astype(jnp.float32)).astype(jnp.bfloat16)
    update_line = [(k, share(deltas.at[core, xy, z], line_peer(k))) for k in far_first]
    update_plane, update_pair = [], []

    def spread(at_z):
        row = deltas.at[core, xy, at_z]
        for p in diagonal_first:
            update_plane.append((p, at_z, share(row, plane_peer(p))))
        update_pair.append((xy, at_z, share(row, partner)))

    def put_sum(sums, values, side, at, j):
        sums[(side * plane + at) * line + j] = jnp.sum(values * values, axis=0)

    def weight_sums(side, at):
        for j in range(line):
            put_sum(wsums, masters[side, at, j], side, at, j)

    def update_sum(side, at, j):
        values = guesses[side, at, j].astype(jnp.float32) + deltas[side, at, j].astype(jnp.float32)
        put_sum(usums, values, side, at, j)

    spread(z)
    mine[...] = update
    m1_new[...] = new_m1
    m2_new[...] = new_m2
    weight_sums(core, xy)
    for turn, (k, copy) in enumerate(reversed(update_line)):
        copy.wait_recv()
        spread(flipped(z, k))
        if turn == line - 3:
            for p in diagonal_first:
                for early_copy in early_plane[p]:
                    early_copy.wait_recv()
                at = flipped(xy, p)
                early_pair[p] = [share(table.at[core, at], partner) for table in early]
                weight_sums(core, at)
    for j in range(line):
        update_sum(core, xy, j)
    for p, at_z, copy in update_plane:
        copy.wait_recv()
        at = flipped(xy, p)
        update_pair.append((at, at_z, share(deltas.at[core, at, at_z], partner)))
        update_sum(core, at, at_z)

    for p in [0] + diagonal_first:
        for copy in early_pair[p]:
            copy.wait_recv()
        weight_sums(other, flipped(xy, p))
    rows_load.wait()

    index0 = lax.broadcasted_iota(jnp.int32, (count, count), 0)
    index1 = lax.broadcasted_iota(jnp.int32, (count, count), 1)

    def tensor_of(index):
        natural = (index % line * plane + index // line % plane) * 2 + index // (line * plane)
        end = jnp.int32(0)
        tensor = jnp.zeros(index.shape, jnp.int32)
        for k in range(rows_ref.shape[0]):
            end = end + rows_ref[k]
            tensor = tensor + (natural >= end).astype(jnp.int32)
        return tensor

    same = tensor_of(index0) == tensor_of(index1)

    def over_tensor(sums):
        per_row = jnp.sum(jnp.sum(sums[...], axis=1), axis=1, keepdims=True)
        return jnp.sum(jnp.where(same, per_row, 0.0), axis=0, keepdims=True)

    wsq = over_tensor(wsums)

    for at, at_z, copy in update_pair:
        copy.wait_recv()
        update_sum(other, at, at_z)

    ratio = jnp.sqrt(wsq / (over_tensor(usums) + 1e-06))
    column = jnp.sum(jnp.where(index0 == index1, ratio, 0.0), axis=1, keepdims=True)
    ratios[...] = jnp.broadcast_to(0.2 * column, (count, LANES))
    for copy in sent:
        copy.wait_send()


def finish(
    line, plane,
    masters, guesses, deltas, ratios, m1_new, m2_new, mine,
    weights_out, master_out, moment1_out, moment2_out,
    weights, master_new, sem,
):
    me = lax.axis_index("dp")
    copies = [
        pltpu.make_async_copy(m1_new, moment1_out, sem.at[0]),
        pltpu.make_async_copy(m2_new, moment2_out, sem.at[1]),
    ]
    for copy in copies:
        copy.start()

    def scale(side, at, j):
        return ratios[pl.ds((side * plane + at) * line + j, 1), :]

    place = (me % 2, me // 2 % plane, me // (2 * plane))
    master_new[...] = masters[place] - scale(*place) * mine[...]
    copies.append(pltpu.make_async_copy(master_new, master_out, sem.at[2]))
    copies[-1].start()

    @pl.loop(0, line)
    def _(j):
        for at in range(plane):
            for side in range(2):
                update = guesses[side, at, j].astype(jnp.float32) + deltas[side, at, j].astype(jnp.float32)
                new_row = masters[side, at, j] - scale(side, at, j) * update
                weights[j, at, side] = new_row.astype(jnp.bfloat16)
        pltpu.make_async_copy(weights.at[j], weights_out.at[j], sem.at[3 + j]).start()

    for j in range(line):
        copies.append(pltpu.make_async_copy(weights.at[j], weights_out.at[j], sem.at[3 + j]))
    for copy in copies:
        copy.wait()


def pinned(array):
    return pltpu.with_memory_space_constraint(array, pltpu.HBM)


def body(grads, master, moment1, moment2, tensor_rows, step_count):
    count = lax.axis_size("dp")
    line, plane = levels(count)
    row = (master.shape[0] // (8 * LANES), 8, LANES)
    f32, bf16 = jnp.float32, jnp.bfloat16
    hbm = pl.BlockSpec(memory_space=pltpu.HBM)
    vmem = pl.BlockSpec(memory_space=pltpu.VMEM)
    table = (2, plane, line) + row
    gathered = line - 1 + line * (plane - 1)
    remotes = line + gathered + 2 * gathered + 2 * plane + gathered + line * plane
    state = pl.pallas_call(
        functools.partial(kernel, count, line, plane),
        out_shape=(
            jax.ShapeDtypeStruct(table, f32),
            jax.ShapeDtypeStruct(table, bf16),
            jax.ShapeDtypeStruct(table, bf16),
            jax.ShapeDtypeStruct((count, LANES), f32),
            jax.ShapeDtypeStruct(row, f32),
            jax.ShapeDtypeStruct(row, f32),
            jax.ShapeDtypeStruct(row, f32),
        ),
        in_specs=[hbm] * 5 + [pl.BlockSpec(memory_space=pltpu.SMEM)],
        out_specs=(vmem,) * 7,
        scratch_shapes=[
            pltpu.VMEM((line, plane) + row, f32),
            pltpu.VMEM((line, plane) + row, f32),
            pltpu.VMEM((line, plane) + row, bf16),
            pltpu.VMEM((line, plane) + row, bf16),
            pltpu.VMEM((line, plane - 1) + row, bf16),
            pltpu.VMEM((line, plane - 1) + row, bf16),
            pltpu.VMEM((line - 1,) + row, bf16),
            pltpu.VMEM((line - 1,) + row, bf16),
            pltpu.VMEM(row, f32),
            pltpu.VMEM(row, f32),
            pltpu.VMEM((count, 8, LANES), f32),
            pltpu.VMEM((count, 8, LANES), f32),
            pltpu.SMEM(tensor_rows.shape, jnp.int32),
            pltpu.SemaphoreType.DMA((2 * line + 4,)),
            pltpu.SemaphoreType.DMA((remotes,)),
            pltpu.SemaphoreType.DMA((remotes,)),
        ],
        compiler_params=pltpu.CompilerParams(
            collective_id=0, has_side_effects=True, vmem_limit_bytes=40 * 1024 * 1024
        ),
        name="exchange",
    )(
        pinned(grads.reshape((line, plane, 2) + row)),
        pinned(master.reshape(row)), pinned(moment1.reshape(row)), pinned(moment2.reshape(row)),
        pinned(tensor_rows), step_count,
    )
    outs = pl.pallas_call(
        functools.partial(finish, line, plane),
        out_shape=(
            jax.ShapeDtypeStruct((line, plane, 2) + row, bf16),
            jax.ShapeDtypeStruct(row, f32),
            jax.ShapeDtypeStruct(row, f32),
            jax.ShapeDtypeStruct(row, f32),
        ),
        in_specs=[vmem] * 7,
        out_specs=(hbm,) * 4,
        scratch_shapes=[
            pltpu.VMEM((line, plane, 2) + row, bf16),
            pltpu.VMEM(row, f32),
            pltpu.SemaphoreType.DMA((3 + line,)),
        ],
        compiler_params=pltpu.CompilerParams(vmem_limit_bytes=24 * 1024 * 1024),
        name="finish",
    )(*state)
    return tuple(out.reshape(-1) for out in outs)


def solution(mesh):
    placed = (P("dp", None), P("dp"), P("dp"), P("dp"), P(), P())
    return jax.shard_map(
        body,
        mesh=mesh,
        in_specs=placed,
        out_specs=(P(), P("dp"), P("dp"), P("dp")),
        check_vma=False,
    )
```

profile of v0, /device:TPU:0, one launch (start us, length us, event | category | flops | bytes accessed | tf_op | source)
XLA Modules:
  0.0 24.3 jit_solution(665410321061929484)
XLA Ops:
  1.3 22.1 %exchange.1 = (f32[2,4,4,5,8,128]{5,4,3,2,1,0:T(8,128)S(1)}, bf16[2,4,4,5,8,128]{5,4,3,2,1,0:T(8,128)(2,1)S(1)}, bf16[2,4,4,5,8,128]{5,4,3,2,1,0:T(8,128)(2,1)S(...) custom-call(f32[4,4,2,5,8,128]{5,4,3,2,1,0:T(8,128)} %bitcast.8, ...), custom_call_target="tpu_custom_call" | custom-call | tf_op jit(solution)/shard_map/exchange/pallas_call | solution.py:299
  23.4 0.9 %finish.1 = (bf16[4,4,2,5,8,128]{5,4,3,2,1,0:T(8,128)(2,1)}, f32[5,8,128]{2,1,0:T(8,128)}, f32[5,8,128]{2,1,0:T(8,128)}, f32[5,8,128]{2,1,0:T(8,128)}) custom-call(f32[2,4,4,5,8,128]{5,4,3,2,1,0:T(8,128)S(1)} %get-tuple-element.15.masters, bf16[2,4,4,5,8,128]{5,4,3,2,1,0:T(8,128)(2,1)S(1)} %get-tuple-element.16.guesses, ...), custom_call_target="tpu_custom_call" | custom-call | tf_op jit(solution)/shard_map/finish/pallas_call | solution.py:339
where the time goes:
time: 24.6 us; the launch traced here: 24.3 us
  Pallas kernels  23 us (93%)
  between operations  1.29 us (5%)
    pallas_call x1, Pallas kernels, body(): pl.pallas_call(functools.partial(kernel, count, line, plane), out_shape=(...  22.1 us
    pallas_call x1, Pallas kernels, body(): pl.pallas_call(functools.partial(finish, line, plane), out_shape=(jax.Sha...  0.89 us

commit v1 on v0

v1 whole, which is shorter than its diff:
```python
import functools

import jax
import jax.numpy as jnp
import numpy as np
from jax import lax
from jax.experimental import pallas as pl
from jax.experimental.pallas import tpu as pltpu
from jax.sharding import PartitionSpec as P

LANES = 128
BETA1, BETA2 = 0.9, 0.999
STEP_BITS = 8


def levels(count):
    chips = count // 2
    bits = chips.bit_length() - 1
    plane = 1 << ((bits + 1) // 2)
    return chips // plane, plane


def flipped(value, mask):
    bit = 1
    while bit <= mask:
        if mask & bit:
            value = value + bit * (1 - 2 * (value // bit % 2))
        bit *= 2
    return value


def power(base, step):
    result = jnp.ones(step.shape, jnp.float32)
    for bit in range(STEP_BITS):
        factor = float(np.float32(float(np.float32(base)) ** (2**bit)))
        result = result * jnp.where((step // 2**bit) % 2 == 1, factor, 1.0)
    return result


def kernel(
    count, line, plane,
    grads, master, moment1, moment2, rows_in, step_ref,
    early, deltas, ratios, m1_new, m2_new, mine, kept,
    own, pair_send, pair_recv, plane_send, plane_recv,
    line_send, line_recv, state, grad_ref, wsums, usums, masks, wsq_ref, rows_ref,
    local_sem, send_sem, recv_sem, plane_ready, line_ready, turn,
):
    me = lax.axis_index("dp")
    core = me % 2
    xy = me // 2 % plane
    z = me // (2 * plane)
    partner = me + 1 - 2 * core
    far_first = list(range(line - 1, 0, -1))
    near_first = far_first[::-1]
    others = list(range(plane - 1, 0, -1))
    layers = far_first + [0]
    stops = [0] + near_first
    f32, bf16 = jnp.float32, jnp.bfloat16
    tensors = rows_ref.shape[0]

    def plane_peer(mask):
        return (z * plane + flipped(xy, mask)) * 2 + core

    def line_peer(mask):
        return (flipped(z, mask) * plane + xy) * 2 + core

    def signal(semaphore, peer):
        pl.semaphore_signal(semaphore, inc=1, device_id=(peer,), device_id_type=pl.DeviceIdType.MESH)

    barrier = pltpu.get_barrier_semaphore()
    signal(barrier, partner)
    for p in others:
        pl.when((core == 1) & (flipped(xy, p) > xy))(functools.partial(signal, barrier, plane_peer(p)))
    for k in far_first:
        pl.when(flipped(z, k) > z)(functools.partial(signal, barrier, line_peer(k)))

    def local(source, target, slot):
        copy = pltpu.make_async_copy(source, target, local_sem.at[slot])
        copy.start()
        return copy

    loads = {k: local(grads.at[flipped(z, k)], own.at[k], 2 + k) for k in layers}
    for i, part in enumerate((moment1, moment2, master)):
        local(part, state.at[core, i], 0)
    rows_load = local(rows_in, rows_ref, 1)

    def greet():
        pl.semaphore_wait(barrier, 1 + z + core * xy)
        for p in others:
            pl.when((core == 1) & (flipped(xy, p) < xy))(functools.partial(signal, plane_ready, plane_peer(p)))
        for k in far_first:
            pl.when(flipped(z, k) < z)(functools.partial(signal, line_ready.at[z], line_peer(k)))

    step = jnp.full((8, LANES), step_ref[0], jnp.int32)
    first_scale = 1.0 - power(BETA1, step)
    second_scale = 1.0 - power(BETA2, step)

    def update_of(first, second, weight):
        return (first / first_scale) / (jnp.sqrt(second / second_scale) + 1e-06) + 0.1 * weight

    def make_row():
        ref = state.at[core]
        pltpu.make_async_copy(ref, ref, local_sem.at[0]).wait()
        weight = state[core, 2]
        kept[...] = weight
        high = weight.astype(bf16)
        early[0, 0, core, 0] = high
        early[0, 0, core, 1] = (weight - high.astype(f32)).astype(bf16)
        early[0, 0, core, 2] = update_of(0.9 * state[core, 0], 0.999 * state[core, 1], weight).astype(bf16)

    send_slots, recv_slots = [{}, {}], [{("line", k): k - 1 for k in near_first}, {}]

    def remote(side, to, kind, key, source, target, peer):
        sender = send_slots[side].setdefault(kind, len(send_slots[side]))
        receiver = recv_slots[to].setdefault(key, len(recv_slots[to]))
        pltpu.make_async_remote_copy(
            src_ref=source, dst_ref=target,
            send_sem=send_sem.at[sender], recv_sem=recv_sem.at[receiver],
            device_id=(peer,), device_id_type=pl.DeviceIdType.MESH,
        ).start()

    def wait_for(semaphore, ref):
        pltpu.make_async_copy(ref, ref, semaphore).wait()

    def arrived(side, key, ref):
        slot = recv_slots[side].setdefault(key, len(recv_slots[side]))
        wait_for(recv_sem.at[slot], ref)

    def left(side, kind, ref):
        wait_for(send_sem.at[send_slots[side][kind]], ref)

    def place(k, p):
        return flipped(z, k), flipped(xy, p)

    def put_sums(sums, k, p, values):
        at = (flipped(z, k) * plane + flipped(xy, p)) * 2
        for side in range(2):
            total = jnp.sum(values[side] * values[side], axis=0)
            sums[pl.ds(at + side, 1), :] = jnp.sum(total, axis=0, keepdims=True)

    def tensor_masks():
        rows_load.wait()
        index = lax.broadcasted_iota(jnp.int32, (count, LANES), 0)
        start = jnp.int32(0)
        for k in range(tensors):
            end = start + rows_ref[k]
            masks[k] = ((index >= start) & (index < end)).astype(f32)
            start = end

    def squares(sums):
        values = sums[...]
        parts = [jnp.sum(masks[k] * values, axis=0, keepdims=True) for k in range(tensors)]
        return jnp.sum(jnp.concatenate(parts, axis=0), axis=1, keepdims=True)

    def weight_squares():
        wsq_ref[...] = jnp.broadcast_to(squares(wsums), wsq_ref.shape)

    def weight_sums(k, p):
        weight = early[k, p, :, 0].astype(f32) + early[k, p, :, 1].astype(f32)
        put_sums(wsums, k, p, weight)

    def update_sums(k, p):
        update = early[k, p, :, 2].astype(f32) + deltas[k, p].astype(f32)
        put_sums(usums, k, p, update)

    rest = pl.ds(1, plane - 1)
    later = pl.ds(1, line - 1)

    @pl.when(core == 0)
    def _():
        greet()
        make_row()
        row = early.at[0, 0, 0]
        remote(0, 1, "row", "row", row, row, partner)
        for k in layers:
            loads[k].wait()
            pair_send[k] = own[k].astype(bf16)
            remote(0, 1, "pair", ("pair", k), pair_send.at[k], pair_recv.at[k], partner)
        remote(0, 1, "state", "state", state.at[0], state.at[0], partner)
        tensor_masks()
        arrived(0, "row", early.at[0, 0, 1])

        def spread(k):
            for p in others:
                remote(0, 1, "plane", ("early", k), early.at[k, 0], early.at[k, p], plane_peer(p) + 1)

        pl.semaphore_wait(turn, 1)
        pl.when(z < line - 1)(functools.partial(spread, 0))
        for to in range(line):
            @pl.when(z != to)
            def _():
                pl.when(z < to)(functools.partial(pl.semaphore_wait, line_ready.at[to], 1))
                k = jnp.bitwise_xor(z, to)
                sender = send_slots[0].setdefault("line", len(send_slots[0]))
                pltpu.make_async_remote_copy(
                    src_ref=early.at[0, 0], dst_ref=early.at[k, 0],
                    send_sem=send_sem.at[sender], recv_sem=recv_sem.at[k - 1],
                    device_id=((to * plane + xy) * 2,), device_id_type=pl.DeviceIdType.MESH,
                ).start()

        @pl.when(z == line - 1)
        def _():
            pl.semaphore_wait(turn, 1)
            spread(0)


        weight_sums(0, 0)
        for k in near_first:
            arrived(0, ("line", k), early.at[k, 0])
            spread(k)
            remote(0, 1, "column", ("column", k), early.at[k, 0], early.at[k, 0], partner)
            weight_sums(k, 0)

        arrived(0, "grad", grad_ref.at[0])
        grad = grad_ref[0]
        new_m1 = 0.9 * state[0, 0] + 0.1 * grad
        new_m2 = 0.999 * state[0, 1] + 0.001 * grad * grad
        mine[...] = update_of(new_m1, new_m2, state[0, 2])
        m1_new[...] = new_m1
        m2_new[...] = new_m2
        left(0, "pair", pair_send)
        left(0, "row", row)
        left(0, "state", state.at[0])
        left(0, "line", early.at[later, 0])
        left(0, "plane", early.at[:, rest])
        left(0, "column", early.at[later, 0])
        pl.when(z < line - 1)(functools.partial(pl.semaphore_wait, turn, 1))
        for k in stops:
            arrived(0, ("early", k), early.at[k, rest])
            for p in range(1, plane):
                weight_sums(k, p)
        weight_squares()
        for k in stops:
            arrived(0, ("delta", k), deltas.at[k])
            for p in range(plane):
                update_sums(k, p)

    @pl.when(core == 1)
    def _():
        greet()
        make_row()
        row = early.at[0, 0, 1]
        remote(1, 0, "row", "row", row, row, partner)
        for turn_k, k in enumerate(layers):
            loads[k].wait()
            if turn_k == 0:
                pl.when(xy < plane - 1)(functools.partial(pl.semaphore_wait, plane_ready, plane - 1 - xy))
                signal(turn, partner)
            arrived(1, ("pair", k), pair_recv.at[k])
            for p in others:
                at = flipped(xy, p)
                plane_send[k, p - 1] = (own[k, at] + pair_recv[k, at].astype(f32)).astype(bf16)
                remote(1, 1, "plane", ("plane", k), plane_send.at[k, p - 1], plane_recv.at[k, p - 1], plane_peer(p))

        tensor_masks()

        def pass_early(k):
            arrived(1, ("early", k), early.at[k, rest])
            remote(1, 0, "early", ("early", k), early.at[k, rest], early.at[k, rest], partner)
            if k > 0:
                arrived(1, ("column", k), early.at[k, 0])

        def weigh(k):
            for p in range(plane):
                if (k, p) != (0, 0):
                    weight_sums(k, p)

        def plane_sum(k):
            arrived(1, ("plane", k), plane_recv.at[k])
            total = own[k, xy] + pair_recv[k, xy].astype(f32)
            for p in others:
                total = total + plane_recv[k, p - 1].astype(f32)
            return total

        for to in range(1, line):
            pl.when(z < to)(functools.partial(pl.semaphore_wait, line_ready.at[to], 1))
        for k in far_first:
            line_send[k - 1] = plane_sum(k).astype(bf16)
            remote(1, 1, "line", "line", line_send.at[k - 1], line_recv.at[k - 1], line_peer(k))
            if k == far_first[0]:
                signal(turn, partner)
        grad = plane_sum(0)
        arrived(1, "state", state.at[0])
        arrived(1, "row", early.at[0, 0, 0])
        arrived(1, "line", line_recv)
        for k in far_first:
            grad = grad + line_recv[k - 1].astype(f32)
        grad = grad / jnp.float32(count)
        new_m1 = 0.9 * state[:, 0] + 0.1 * grad
        new_m2 = 0.999 * state[:, 1] + 0.001 * grad * grad
        update = update_of(new_m1, new_m2, state[:, 2])
        deltas[0, 0] = (update - early[0, 0, :, 2].astype(f32)).astype(bf16)
        for k in far_first:
            remote(1, 1, "dline", ("dline", k), deltas.at[0, 0], deltas.at[k, 0], line_peer(k))

        def spread(k):
            for p in others:
                remote(1, 1, "dplane", ("dplane", k), deltas.at[k, 0], deltas.at[k, p], plane_peer(p))

        spread(0)
        grad_ref[...] = grad
        remote(1, 0, "grad", "grad", grad_ref.at[0], grad_ref.at[0], partner)
        mine[...] = update[1]
        m1_new[...] = new_m1[1]
        m2_new[...] = new_m2[1]
        weight_sums(0, 0)
        left(1, "row", row)
        left(1, "plane", plane_send)
        left(1, "line", line_send)
        for k in near_first:
            arrived(1, ("dline", k), deltas.at[k, 0])
            spread(k)
            if k == near_first[0]:
                pass_early(0)
        for k in stops:
            if k > 0:
                pass_early(k)
            weigh(k)
        weight_squares()
        for k in stops:
            arrived(1, ("dplane", k), deltas.at[k, rest])
            remote(1, 0, "delta", ("delta", k), deltas.at[k], deltas.at[k], partner)
            for p in range(plane):
                update_sums(k, p)
        left(1, "grad", grad_ref.at[0])
        left(1, "dline", deltas.at[later, 0])
        left(1, "dplane", deltas.at[:, rest])
        left(1, "delta", deltas)
        left(1, "early", early.at[:, rest])

    ratio = 0.2 * jnp.sqrt(wsq_ref[...] / (squares(usums) + 1e-06))
    row_ratio = masks[0] * ratio[0:1]
    for k in range(1, tensors):
        row_ratio = row_ratio + masks[k] * ratio[k:k + 1]
    ratios[...] = row_ratio
    assert max(map(len, send_slots)) <= send_sem.shape[0]
    assert max(map(len, recv_slots)) <= recv_sem.shape[0]


def finish(
    line, plane,
    early, deltas, ratios, m1_new, m2_new, mine, kept,
    weights_out, master_out, moment1_out, moment2_out,
    weights, master_new, sem,
):
    me = lax.axis_index("dp")
    z, xy, core = me // (2 * plane), me // 2 % plane, me % 2
    copies = [
        pltpu.make_async_copy(m1_new, moment1_out, sem.at[0]),
        pltpu.make_async_copy(m2_new, moment2_out, sem.at[1]),
    ]
    for copy in copies:
        copy.start()

    def scale(j, at, side):
        return ratios[pl.ds((j * plane + at) * 2 + side, 1), :]

    master_new[...] = kept[...] - scale(z, xy, core) * mine[...]
    copies.append(pltpu.make_async_copy(master_new, master_out, sem.at[2]))
    copies[-1].start()

    def layer_copy(j):
        return pltpu.make_async_copy(weights.at[j], weights_out.at[j], sem.at[3 + j])

    @pl.loop(0, line)
    def _(k):
        j = jnp.bitwise_xor(z, k)
        for p in range(plane):
            at = flipped(xy, p)
            for side in range(2):
                high, low, guess = (early[k, p, side, i].astype(jnp.float32) for i in range(3))
                update = guess + deltas[k, p, side].astype(jnp.float32)
                new_row = (high + low) - scale(j, at, side) * update
                weights[j, at, side] = new_row.astype(jnp.bfloat16)
        layer_copy(j).start()

    for j in range(line):
        copies.append(layer_copy(j))
    for copy in copies:
        copy.wait()


def pinned(array):
    return pltpu.with_memory_space_constraint(array, pltpu.HBM)


def body(grads, master, moment1, moment2, tensor_rows, step_count):
    count = lax.axis_size("dp")
    line, plane = levels(count)
    row = (master.shape[0] // (8 * LANES), 8, LANES)
    f32, bf16 = jnp.float32, jnp.bfloat16
    hbm = pl.BlockSpec(memory_space=pltpu.HBM)
    vmem = pl.BlockSpec(memory_space=pltpu.VMEM)
    pair = (2,) + row
    table = (line, plane) + pair
    kept = jax.ShapeDtypeStruct(row, f32)
    state = pl.pallas_call(
        functools.partial(kernel, count, line, plane),
        out_shape=(
            jax.ShapeDtypeStruct((line, plane, 2, 3) + row, bf16),
            jax.ShapeDtypeStruct(table, bf16),
            jax.ShapeDtypeStruct((count, LANES), f32),
            kept, kept, kept, kept,
        ),
        in_specs=[hbm] * 5 + [pl.BlockSpec(memory_space=pltpu.SMEM)],
        out_specs=(vmem,) * 7,
        scratch_shapes=[
            pltpu.VMEM(table, f32),
            pltpu.VMEM(table, bf16),
            pltpu.VMEM(table, bf16),
            pltpu.VMEM((line, plane - 1) + pair, bf16),
            pltpu.VMEM((line, plane - 1) + pair, bf16),
            pltpu.VMEM((line - 1,) + pair, bf16),
            pltpu.VMEM((line - 1,) + pair, bf16),
            pltpu.VMEM((2, 3) + row, f32),
            pltpu.VMEM(pair, f32),
            pltpu.VMEM((count, LANES), f32),
            pltpu.VMEM((count, LANES), f32),
            pltpu.VMEM((tensor_rows.shape[0], count, LANES), f32),
            pltpu.VMEM((tensor_rows.shape[0], LANES), f32),
            pltpu.SMEM(tensor_rows.shape, jnp.int32),
            pltpu.SemaphoreType.DMA((line + 2,)),
            pltpu.SemaphoreType.DMA((8,)),
            pltpu.SemaphoreType.DMA((6 * line + 1,)),
            pltpu.SemaphoreType.REGULAR,
            pltpu.SemaphoreType.REGULAR((line,)),
            pltpu.SemaphoreType.REGULAR,
        ],
        compiler_params=pltpu.CompilerParams(
            collective_id=0, has_side_effects=True, vmem_limit_bytes=48 * 1024 * 1024
        ),
        name="exchange",
    )(
        pinned(grads.reshape(table)),
        pinned(master.reshape(row)), pinned(moment1.reshape(row)), pinned(moment2.reshape(row)),
        pinned(tensor_rows), step_count,
    )
    outs = pl.pallas_call(
        functools.partial(finish, line, plane),
        out_shape=(jax.ShapeDtypeStruct(table, bf16), kept, kept, kept),
        in_specs=[vmem] * 7,
        out_specs=(hbm,) * 4,
        scratch_shapes=[
            pltpu.VMEM(table, bf16),
            pltpu.VMEM(row, f32),
            pltpu.SemaphoreType.DMA((3 + line,)),
        ],
        compiler_params=pltpu.CompilerParams(vmem_limit_bytes=24 * 1024 * 1024),
        name="finish",
    )(*state)
    return tuple(out.reshape(-1) for out in outs)


def solution(mesh):
    placed = (P("dp", None), P("dp"), P("dp"), P("dp"), P(), P())
    return jax.shard_map(
        body,
        mesh=mesh,
        in_specs=placed,
        out_specs=(P(), P("dp"), P("dp"), P("dp")),
        check_vma=False,
    )
```

time: 24.6 us -> 21.2 us (0.86)
  Pallas kernels: 23 us -> 19.8 us
    pallas_call x1, Pallas kernels: 22.1 us -> 18.8 us  [body(): pl.pallas_call(functools.partial(kernel, count, line, plane), out_shape=(...]
where the time goes in v1:
time: 21.2 us; the launch traced here: 21 us
  Pallas kernels  19.8 us (93%)
  between operations  1.29 us (6%)
    pallas_call x1, Pallas kernels, body(): pl.pallas_call(functools.partial(kernel, count, line, plane), out_shape=(...  18.8 us
    pallas_call x1, Pallas kernels, body(): pl.pallas_call(functools.partial(finish, line, plane), out_shape=(jax.Sha...  0.94 us

profile of v1, /device:TPU:0, one launch (start us, length us, event | category | flops | bytes accessed | tf_op | source)
XLA Modules:
  0.0 21.0 jit_solution(1780641716506610229)
XLA Ops:
  1.3 18.8 %exchange.1 = (bf16[4,4,2,3,5,8,128]{6,5,4,3,2,1,0:T(8,128)(2,1)S(1)}, bf16[4,4,2,5,8,128]{5,4,3,2,1,0:T(8,128)(2,1)S(1)}, f32[32,128]{1,0:T(8,128)S(1)}, f32[5,...) custom-call(f32[4,4,2,5,8,128]{5,4,3,2,1,0:T(8,128)} %bitcast.8, ...), custom_call_target="tpu_custom_call" | custom-call | tf_op jit(solution)/shard_map/exchange/pallas_call | solution.py:397
  20.1 0.9 %finish.1 = (bf16[4,4,2,5,8,128]{5,4,3,2,1,0:T(8,128)(2,1)}, f32[5,8,128]{2,1,0:T(8,128)}, f32[5,8,128]{2,1,0:T(8,128)}, f32[5,8,128]{2,1,0:T(8,128)}) custom-call(bf16[4,4,2,3,5,8,128]{6,5,4,3,2,1,0:T(8,128)(2,1)S(1)} %get-tuple-element.15.early, bf16[4,4,2,5,8,128]{5,4,3,2,1,0:T(8,128)(2,1)S(1)} %get-tuple-element.16.deltas, ...), custom_call_target="tpu_custom_call" | custom-call | tf_op jit(solution)/shard_map/finish/pallas_call | solution.py:438

commit v2 on v1

v2 whole, which is shorter than its diff:
```python
import functools
import math

import jax
import jax.numpy as jnp
import numpy as np
from jax import lax
from jax.experimental import pallas as pl
from jax.experimental.pallas import tpu as pltpu
from jax.sharding import PartitionSpec as P

LANES = 128
BETA1, BETA2 = 0.9, 0.999
STEP_BITS = 8


def levels(count):
    chips = count // 2
    bits = chips.bit_length() - 1
    plane = 1 << ((bits + 1) // 2)
    return chips // plane, plane


def flipped(value, mask):
    bit = 1
    while bit <= mask:
        if mask & bit:
            value = value + bit * (1 - 2 * (value // bit % 2))
        bit *= 2
    return value


def power(base, step):
    result = jnp.ones(step.shape, jnp.float32)
    for bit in range(STEP_BITS):
        factor = float(np.float32(float(np.float32(base)) ** (2**bit)))
        result = result * jnp.where((step // 2**bit) % 2 == 1, factor, 1.0)
    return result


def kernel(
    count, line, plane,
    grads, master, moment1, moment2, rows_in, step_ref,
    weights, updates, ratios, m1_new, m2_new, mine, kept,
    early, deltas, leaving, own, pair_send, pair_recv, plane_send, plane_recv,
    line_send, line_recv, state, grad_ref, wsums, usums, masks, wsq_ref, rows_ref,
    sems, plane_ready, line_ready, turn,
):
    me = lax.axis_index("dp")
    core = me % 2
    xy = me // 2 % plane
    z = me // (2 * plane)
    partner = me + 1 - 2 * core
    far_first = list(range(line - 1, 0, -1))
    near_first = far_first[::-1]
    others = list(range(plane - 1, 0, -1))
    order = sorted(near_first, key=lambda k: (bin(k).count("1"), -k))
    layers = order + [0]
    stops = [0] + near_first
    f32, bf16 = jnp.float32, jnp.bfloat16
    tensors = rows_ref.shape[0]

    def plane_peer(mask):
        return (z * plane + flipped(xy, mask)) * 2 + core

    def line_peer(mask):
        return (flipped(z, mask) * plane + xy) * 2 + core

    def signal(semaphore, peer):
        pl.semaphore_signal(semaphore, inc=1, device_id=(peer,), device_id_type=pl.DeviceIdType.MESH)

    barrier = pltpu.get_barrier_semaphore()
    signal(barrier, partner)
    for p in others:
        pl.when((core == 1) & (flipped(xy, p) > xy))(functools.partial(signal, barrier, plane_peer(p)))
    for k in far_first:
        pl.when(flipped(z, k) > z)(functools.partial(signal, barrier, line_peer(k)))

    def local(source, target, slot):
        copy = pltpu.make_async_copy(source, target, sems.at[slot])
        copy.start()
        return copy

    loads = {k: local(grads.at[flipped(z, k)], own.at[k], k) for k in layers}
    for i, part in enumerate((moment1, moment2, master)):
        local(part, state.at[core, i], 4 * line + 2)
    rows_load = local(rows_in, rows_ref, 4 * line + 3)

    def greet():
        pl.semaphore_wait(barrier, 1 + z + core * xy)
        for p in others:
            pl.when((core == 1) & (flipped(xy, p) < xy))(functools.partial(signal, plane_ready, plane_peer(p)))
        for k in far_first:
            pl.when(flipped(z, k) < z)(functools.partial(signal, line_ready.at[z - 1], line_peer(k)))

    step = jnp.full((8, LANES), step_ref[0], jnp.int32)
    first_scale = 1.0 - power(BETA1, step)
    second_scale = 1.0 - power(BETA2, step)

    def update_of(first, second, weight):
        return (first / first_scale) / (jnp.sqrt(second / second_scale) + 1e-06) + 0.1 * weight

    def make_row():
        ref = state.at[core]
        pltpu.make_async_copy(ref, ref, sems.at[4 * line + 2]).wait()
        weight = state[core, 2]
        kept[...] = weight
        high = weight.astype(bf16)
        early[0, 0, core, 0] = high
        early[0, 0, core, 1] = (weight - high.astype(f32)).astype(bf16)
        early[0, 0, core, 2] = update_of(0.9 * state[core, 0], 0.999 * state[core, 1], weight).astype(bf16)

    pools = {
        0: {"row": 2 * line, "grad": 3 * line, "delta": 0, "early": line, "line": 2 * line},
        1: {"row": 4 * line + 1, "state": 4 * line + 1, "line": 4 * line, "pair": line, "plane": 2 * line,
            "dplane": 0, "dline": line, "early": 3 * line},
    }
    sent = [0, 0]

    def remote(side, to, key, source, target, peer):
        name, k = key if isinstance(key, tuple) else (key, 0)
        pltpu.make_async_remote_copy(
            src_ref=source, dst_ref=target,
            send_sem=sems.at[4 * line + 4], recv_sem=sems.at[pools[to][name] + k],
            device_id=(peer,), device_id_type=pl.DeviceIdType.MESH,
        ).start()
        words = 2 if source.dtype == f32 else 1
        sent[side] += words * math.prod(source.shape[:-3])

    def wait_for(semaphore, ref):
        pltpu.make_async_copy(ref, ref, semaphore).wait()

    def arrived(side, key, ref):
        name, k = key if isinstance(key, tuple) else (key, 0)
        wait_for(sems.at[pools[side][name] + k], ref)

    def all_left(side):
        wait_for(sems.at[4 * line + 4], leaving.at[pl.ds(0, sent[side])])

    def place(k, p):
        return flipped(z, k), flipped(xy, p)

    def put_sums(sums, k, p, values):
        at = (flipped(z, k) * plane + flipped(xy, p)) * 2
        for side in range(2):
            total = jnp.sum(values[side] * values[side], axis=0)
            sums[pl.ds(at + side, 1), :] = jnp.sum(total, axis=0, keepdims=True)

    def tensor_masks():
        rows_load.wait()
        index = lax.broadcasted_iota(jnp.int32, (count, LANES), 0)
        start = jnp.int32(0)
        for k in range(tensors):
            end = start + rows_ref[k]
            masks[k] = ((index >= start) & (index < end)).astype(f32)
            start = end

    def squares(sums):
        values = sums[...]
        parts = [jnp.sum(masks[k] * values, axis=0, keepdims=True) for k in range(tensors)]
        return jnp.sum(jnp.concatenate(parts, axis=0), axis=1, keepdims=True)

    def weight_squares():
        wsq_ref[...] = jnp.broadcast_to(squares(wsums), wsq_ref.shape)

    def weight_sums(k, p):
        weight = early[k, p, :, 0].astype(f32) + early[k, p, :, 1].astype(f32)
        weights[place(k, p)] = weight
        put_sums(wsums, k, p, weight)

    def update_sums(k, p):
        update = early[k, p, :, 2].astype(f32) + deltas[k, p].astype(f32)
        updates[place(k, p)] = update
        put_sums(usums, k, p, update)

    rest = pl.ds(1, plane - 1)
    later = pl.ds(1, line - 1)

    @pl.when(core == 0)
    def _():
        greet()
        make_row()
        row = early.at[0, 0, 0]
        remote(0, 1, "row", row, row, partner)
        for k in layers:
            loads[k].wait()
            pair_send[k] = own[k].astype(bf16)
            remote(0, 1, ("pair", k), pair_send.at[k], pair_recv.at[k], partner)
        remote(0, 1, "state", state.at[0], state.at[0], partner)
        tensor_masks()
        arrived(0, "row", early.at[0, 0, 1])

        def spread(k):
            for p in others:
                remote(0, 1, ("early", k), early.at[k, 0], early.at[k, p], plane_peer(p) + 1)

        for to in range(line):
            @pl.when(z != to)
            def _():
                if to > 0:
                    pl.when(z < to)(functools.partial(pl.semaphore_wait, line_ready.at[to - 1], 1))
                k = jnp.bitwise_xor(z, to)
                remote(0, 0, ("line", k), early.at[0, 0], early.at[k, 0], (to * plane + xy) * 2)

        sent[0] -= math.prod(early.shape[2:4])

        pl.semaphore_wait(turn, 1)
        spread(0)
        weight_sums(0, 0)
        for k in near_first:
            arrived(0, ("line", k), early.at[k, 0])
            spread(k)
            remote(0, 1, ("early", k), early.at[k, 0], early.at[k, 0], partner)
            weight_sums(k, 0)

        arrived(0, "grad", grad_ref.at[0])
        grad = grad_ref[0]
        new_m1 = 0.9 * state[0, 0] + 0.1 * grad
        new_m2 = 0.999 * state[0, 1] + 0.001 * grad * grad
        mine[...] = update_of(new_m1, new_m2, state[0, 2])
        m1_new[...] = new_m1
        m2_new[...] = new_m2
        for k in stops:
            arrived(0, ("early", k), early.at[k, rest])
            for p in range(1, plane):
                weight_sums(k, p)
        weight_squares()
        for k in stops:
            arrived(0, ("delta", k), deltas.at[k])
            for p in range(plane):
                update_sums(k, p)
        all_left(0)

    @pl.when(core == 1)
    def _():
        greet()
        make_row()
        row = early.at[0, 0, 1]
        remote(1, 0, "row", row, row, partner)
        for turn_k, k in enumerate(layers):
            loads[k].wait()
            if turn_k == 0:
                pl.when(xy < plane - 1)(functools.partial(pl.semaphore_wait, plane_ready, plane - 1 - xy))
            arrived(1, ("pair", k), pair_recv.at[k])
            for p in others:
                at = flipped(xy, p)
                plane_send[k, p - 1] = (own[k, at] + pair_recv[k, at].astype(f32)).astype(bf16)
                remote(1, 1, ("plane", k), plane_send.at[k, p - 1], plane_recv.at[k, p - 1], plane_peer(p))

        tensor_masks()

        def pass_early(k):
            arrived(1, ("early", k), early.at[k] if k > 0 else early.at[k, rest])
            remote(1, 0, ("early", k), early.at[k, rest], early.at[k, rest], partner)

        def weigh(k):
            for p in range(plane):
                if (k, p) != (0, 0):
                    weight_sums(k, p)

        def plane_sum(k):
            arrived(1, ("plane", k), plane_recv.at[k])
            total = own[k, xy] + pair_recv[k, xy].astype(f32)
            for p in others:
                total = total + plane_recv[k, p - 1].astype(f32)
            return total

        for to in range(1, line):
            pl.when(z < to)(functools.partial(pl.semaphore_wait, line_ready.at[to - 1], 1))
        for k in order:
            line_send[k - 1] = plane_sum(k).astype(bf16)
            remote(1, 1, "line", line_send.at[k - 1], line_recv.at[k - 1], line_peer(k))
            if k == order[0]:
                signal(turn, partner)
        grad = plane_sum(0)
        arrived(1, "row", early.at[0, pl.ds(0, 3), 0])
        arrived(1, "line", line_recv)
        for k in far_first:
            grad = grad + line_recv[k - 1].astype(f32)
        grad = grad / jnp.float32(count)
        new_m1 = 0.9 * state[:, 0] + 0.1 * grad
        new_m2 = 0.999 * state[:, 1] + 0.001 * grad * grad
        update = update_of(new_m1, new_m2, state[:, 2])
        deltas[0, 0] = (update - early[0, 0, :, 2].astype(f32)).astype(bf16)
        for k in far_first:
            remote(1, 1, ("dline", k), deltas.at[0, 0], deltas.at[k, 0], line_peer(k))

        def spread(k):
            for p in others:
                remote(1, 1, ("dplane", k), deltas.at[k, 0], deltas.at[k, p], plane_peer(p))

        spread(0)
        grad_ref[...] = grad
        remote(1, 0, "grad", grad_ref.at[0], grad_ref.at[0], partner)
        mine[...] = update[1]
        m1_new[...] = new_m1[1]
        m2_new[...] = new_m2[1]
        weight_sums(0, 0)
        for k in near_first:
            arrived(1, ("dline", k), deltas.at[k, 0])
            spread(k)
            if k == near_first[0]:
                pass_early(0)
        for k in stops:
            if k > 0:
                pass_early(k)
            weigh(k)
        weight_squares()
        for k in stops:
            arrived(1, ("dplane", k), deltas.at[k, rest])
            remote(1, 0, ("delta", k), deltas.at[k], deltas.at[k], partner)
            for p in range(plane):
                update_sums(k, p)
        all_left(1)

    ratio = 0.2 * jnp.sqrt(wsq_ref[...] / (squares(usums) + 1e-06))
    row_ratio = masks[0] * ratio[0:1]
    for k in range(1, tensors):
        row_ratio = row_ratio + masks[k] * ratio[k:k + 1]
    ratios[...] = row_ratio


def finish(
    line, plane,
    weights, updates, ratios, m1_new, m2_new, mine, kept,
    weights_out, master_out, moment1_out, moment2_out,
    rounded, master_new, sem,
):
    me = lax.axis_index("dp")
    copies = [
        pltpu.make_async_copy(m1_new, moment1_out, sem.at[0]),
        pltpu.make_async_copy(m2_new, moment2_out, sem.at[1]),
    ]
    for copy in copies:
        copy.start()
    master_new[...] = kept[...] - ratios[pl.ds(me, 1), :] * mine[...]
    copies.append(pltpu.make_async_copy(master_new, master_out, sem.at[2]))
    copies[-1].start()

    def layer_copy(j):
        return pltpu.make_async_copy(rounded.at[j], weights_out.at[j], sem.at[3 + j])

    @pl.loop(0, line)
    def _(j):
        for at in range(plane):
            for side in range(2):
                scale = ratios[pl.ds((j * plane + at) * 2 + side, 1), :]
                new_row = weights[j, at, side] - scale * updates[j, at, side]
                rounded[j, at, side] = new_row.astype(jnp.bfloat16)
        layer_copy(j).start()

    for j in range(line):
        copies.append(layer_copy(j))
    for copy in copies:
        copy.wait()


def pinned(array):
    return pltpu.with_memory_space_constraint(array, pltpu.HBM)


def body(grads, master, moment1, moment2, tensor_rows, step_count):
    count = lax.axis_size("dp")
    line, plane = levels(count)
    row = (master.shape[0] // (8 * LANES), 8, LANES)
    f32, bf16 = jnp.float32, jnp.bfloat16
    hbm = pl.BlockSpec(memory_space=pltpu.HBM)
    vmem = pl.BlockSpec(memory_space=pltpu.VMEM)
    pair = (2,) + row
    table = (line, plane) + pair
    kept = jax.ShapeDtypeStruct(row, f32)
    leaving = 12 * line * plane
    state = pl.pallas_call(
        functools.partial(kernel, count, line, plane),
        out_shape=(
            jax.ShapeDtypeStruct(table, f32),
            jax.ShapeDtypeStruct(table, f32),
            jax.ShapeDtypeStruct((count, LANES), f32),
            kept, kept, kept, kept,
        ),
        in_specs=[hbm] * 5 + [pl.BlockSpec(memory_space=pltpu.SMEM)],
        out_specs=(vmem,) * 7,
        scratch_shapes=[
            pltpu.VMEM((line, plane, 2, 3) + row, bf16),
            pltpu.VMEM(table, bf16),
            pltpu.VMEM((leaving,) + row, bf16),
            pltpu.VMEM(table, f32),
            pltpu.VMEM(table, bf16),
            pltpu.VMEM(table, bf16),
            pltpu.VMEM((line, plane - 1) + pair, bf16),
            pltpu.VMEM((line, plane - 1) + pair, bf16),
            pltpu.VMEM((line - 1,) + pair, bf16),
            pltpu.VMEM((line - 1,) + pair, bf16),
            pltpu.VMEM((2, 3) + row, f32),
            pltpu.VMEM(pair, f32),
            pltpu.VMEM((count, LANES), f32),
            pltpu.VMEM((count, LANES), f32),
            pltpu.VMEM((tensor_rows.shape[0], count, LANES), f32),
            pltpu.VMEM((tensor_rows.shape[0], LANES), f32),
            pltpu.SMEM(tensor_rows.shape, jnp.int32),
            pltpu.SemaphoreType.DMA((4 * line + 5,)),
            pltpu.SemaphoreType.REGULAR,
            pltpu.SemaphoreType.REGULAR((line - 1,)),
            pltpu.SemaphoreType.REGULAR,
        ],
        compiler_params=pltpu.CompilerParams(
            collective_id=0, has_side_effects=True, vmem_limit_bytes=min(60, 20 + count // 4) * 1024 * 1024
        ),
        name="exchange",
    )(
        pinned(grads.reshape(table)),
        pinned(master.reshape(row)), pinned(moment1.reshape(row)), pinned(moment2.reshape(row)),
        pinned(tensor_rows), step_count,
    )
    outs = pl.pallas_call(
        functools.partial(finish, line, plane),
        out_shape=(jax.ShapeDtypeStruct(table, bf16), kept, kept, kept),
        in_specs=[vmem] * 7,
        out_specs=(hbm,) * 4,
        scratch_shapes=[
            pltpu.VMEM(table, bf16),
            pltpu.VMEM(row, f32),
            pltpu.SemaphoreType.DMA((3 + line,)),
        ],
        compiler_params=pltpu.CompilerParams(vmem_limit_bytes=24 * 1024 * 1024),
        name="finish",
    )(*state)
    return tuple(out.reshape(-1) for out in outs)


def solution(mesh):
    placed = (P("dp", None), P("dp"), P("dp"), P("dp"), P(), P())
    return jax.shard_map(
        body,
        mesh=mesh,
        in_specs=placed,
        out_specs=(P(), P("dp"), P("dp"), P("dp")),
        check_vma=False,
    )
```

time: 21.2 us -> 20.5 us (0.967)
  Pallas kernels: 19.8 us -> 19 us
    pallas_call x1, Pallas kernels: 18.8 us -> 18.2 us  [body(): pl.pallas_call(functools.partial(kernel, count, line, plane), out_shape=(...]
where the time goes in v2:
time: 20.5 us; the launch traced here: 20.3 us
  Pallas kernels  19 us (93%)
  between operations  1.29 us (6%)
    pallas_call x1, Pallas kernels, body(): pl.pallas_call(functools.partial(kernel, count, line, plane), out_shape=(...  18.2 us
    pallas_call x1, Pallas kernels, body(): pl.pallas_call(functools.partial(finish, line, plane), out_shape=(jax.Sha...  0.81 us

profile of v2, /device:TPU:0, one launch (start us, length us, event | category | flops | bytes accessed | tf_op | source)
XLA Modules:
  0.0 20.3 jit_solution(4170965906404126472)
XLA Ops:
  1.3 18.2 %exchange.1 = (f32[4,4,2,5,8,128]{5,4,3,2,1,0:T(8,128)S(1)}, f32[4,4,2,5,8,128]{5,4,3,2,1,0:T(8,128)S(1)}, f32[32,128]{1,0:T(8,128)S(1)}, f32[5,8,128]{2,1,0:T(8...) custom-call(f32[4,4,2,5,8,128]{5,4,3,2,1,0:T(8,128)} %bitcast.8, ...), custom_call_target="tpu_custom_call" | custom-call | tf_op jit(solution)/shard_map/exchange/pallas_call | solution.py:373
  19.5 0.8 %finish.1 = (bf16[4,4,2,5,8,128]{5,4,3,2,1,0:T(8,128)(2,1)}, f32[5,8,128]{2,1,0:T(8,128)}, f32[5,8,128]{2,1,0:T(8,128)}, f32[5,8,128]{2,1,0:T(8,128)}) custom-call(f32[4,4,2,5,8,128]{5,4,3,2,1,0:T(8,128)S(1)} %get-tuple-element.15.weights, f32[4,4,2,5,8,128]{5,4,3,2,1,0:T(8,128)S(1)} %get-tuple-element.16.updates, f32[32,128]{1,0:T(8,128)S(1)} %get-tuple-element.17.ratios, ...), custom_call_target="tpu_custom_call" | custom-call | tf_op jit(solution)/shard_map/finish/pallas_call | solution.py:415

commit v3 on v2

--- a/solution.py
+++ b/solution.py
@@ -57,6 +57,7 @@
     order = sorted(near_first, key=lambda k: (bin(k).count("1"), -k))
     layers = order + [0]
     stops = [0] + near_first
+    far = list(range(line // 2, line))
     f32, bf16 = jnp.float32, jnp.bfloat16
     tensors = rows_ref.shape[0]
 
@@ -248,6 +249,9 @@
                 remote(1, 1, ("plane", k), plane_send.at[k, p - 1], plane_recv.at[k, p - 1], plane_peer(p))
 
         tensor_masks()
+        all_left(1)
+        sent[1] = 0
+        signal(turn, partner)
 
         def pass_early(k):
             arrived(1, ("early", k), early.at[k] if k > 0 else early.at[k, rest])
@@ -270,8 +274,6 @@
         for k in order:
             line_send[k - 1] = plane_sum(k).astype(bf16)
             remote(1, 1, "line", line_send.at[k - 1], line_recv.at[k - 1], line_peer(k))
-            if k == order[0]:
-                signal(turn, partner)
         grad = plane_sum(0)
         arrived(1, "row", early.at[0, pl.ds(0, 3), 0])
         arrived(1, "line", line_recv)
@@ -289,6 +291,11 @@
             for p in others:
                 remote(1, 1, ("dplane", k), deltas.at[k, 0], deltas.at[k, p], plane_peer(p))
 
+        def spread_both(k):
+            for p in others:
+                remote(1, 0, ("delta", k), deltas.at[k, 0], deltas.at[k, p], plane_peer(p) - 1)
+            remote(1, 0, ("delta", k), deltas.at[k, 0], deltas.at[k, 0], partner)
+
         spread(0)
         grad_ref[...] = grad
         remote(1, 0, "grad", grad_ref.at[0], grad_ref.at[0], partner)
@@ -296,11 +303,18 @@
         m1_new[...] = new_m1[1]
         m2_new[...] = new_m2[1]
         weight_sums(0, 0)
-        for k in near_first:
-            arrived(1, ("dline", k), deltas.at[k, 0])
-            spread(k)
-            if k == near_first[0]:
+        for turn_k, of in enumerate(near_first + [0]):
+            @pl.when(z != of)
+            def _():
+                k = jnp.bitwise_xor(z, of)
+                arrived(1, ("dline", k), deltas.at[k, 0])
+                if of in far:
+                    pl.when(z == 0)(functools.partial(spread_both, of))
+                spread(k)
+
+            if turn_k == 0:
                 pass_early(0)
+        sent[1] -= (len(others) + len(far) * plane) * 2
         for k in stops:
             if k > 0:
                 pass_early(k)
@@ -308,7 +322,11 @@
         weight_squares()
         for k in stops:
             arrived(1, ("dplane", k), deltas.at[k, rest])
-            remote(1, 0, ("delta", k), deltas.at[k], deltas.at[k], partner)
+            hand_on = functools.partial(remote, 1, 0, ("delta", k), deltas.at[k], deltas.at[k], partner)
+            if k in far:
+                pl.when(z > 0)(hand_on)
+            else:
+                hand_on()
             for p in range(plane):
                 update_sums(k, p)
         all_left(1)

time: 20.5 us -> 20.4 us (level)
  no operation moved by 1% of the time
where the time goes in v3:
time: 20.4 us; the launch traced here: 20.2 us
  Pallas kernels  18.9 us (93%)
  between operations  1.29 us (6%)
    pallas_call x1, Pallas kernels, body(): pl.pallas_call(functools.partial(kernel, count, line, plane), out_shape=(...  18.1 us
    pallas_call x1, Pallas kernels, body(): pl.pallas_call(functools.partial(finish, line, plane), out_shape=(jax.Sha...  0.81 us

profile of v3, /device:TPU:0, one launch (start us, length us, event | category | flops | bytes accessed | tf_op | source)
XLA Modules:
  0.0 20.2 jit_solution(10914351974412553367)
XLA Ops:
  1.3 18.1 %exchange.1 = (f32[4,4,2,5,8,128]{5,4,3,2,1,0:T(8,128)S(1)}, f32[4,4,2,5,8,128]{5,4,3,2,1,0:T(8,128)S(1)}, f32[32,128]{1,0:T(8,128)S(1)}, f32[5,8,128]{2,1,0:T(8...) custom-call(f32[4,4,2,5,8,128]{5,4,3,2,1,0:T(8,128)} %bitcast.8, ...), custom_call_target="tpu_custom_call" | custom-call | tf_op jit(solution)/shard_map/exchange/pallas_call | solution.py:391
  19.4 0.8 %finish.1 = (bf16[4,4,2,5,8,128]{5,4,3,2,1,0:T(8,128)(2,1)}, f32[5,8,128]{2,1,0:T(8,128)}, f32[5,8,128]{2,1,0:T(8,128)}, f32[5,8,128]{2,1,0:T(8,128)}) custom-call(f32[4,4,2,5,8,128]{5,4,3,2,1,0:T(8,128)S(1)} %get-tuple-element.15.weights, f32[4,4,2,5,8,128]{5,4,3,2,1,0:T(8,128)S(1)} %get-tuple-element.16.updates, f32[32,128]{1,0:T(8,128)S(1)} %get-tuple-element.17.ratios, ...), custom_call_target="tpu_custom_call" | custom-call | tf_op jit(solution)/shard_map/finish/pallas_call | solution.py:433

commit v4 on v3

--- a/solution.py
+++ b/solution.py
@@ -57,7 +57,7 @@
     order = sorted(near_first, key=lambda k: (bin(k).count("1"), -k))
     layers = order + [0]
     stops = [0] + near_first
-    far = list(range(line // 2, line))
+    far = [line - 1]
     f32, bf16 = jnp.float32, jnp.bfloat16
     tensors = rows_ref.shape[0]
 
@@ -208,10 +208,19 @@
         pl.semaphore_wait(turn, 1)
         spread(0)
         weight_sums(0, 0)
+        last = (z == line - 1).astype(jnp.int32)
+        for i in range(line):
+            of = i + last * (line - 2 - 2 * i)
+
+            @pl.when((of != z) & (of >= 0))
+            def _():
+                k = jnp.bitwise_xor(z, of)
+                arrived(0, ("line", k), early.at[k, 0])
+                spread(k)
+                remote(0, 1, ("early", k), early.at[k, 0], early.at[k, 0], partner)
+
+        sent[0] -= plane * math.prod(early.shape[2:4])
         for k in near_first:
-            arrived(0, ("line", k), early.at[k, 0])
-            spread(k)
-            remote(0, 1, ("early", k), early.at[k, 0], early.at[k, 0], partner)
             weight_sums(k, 0)
 
         arrived(0, "grad", grad_ref.at[0])

time: 20.4 us -> 20.1 us (0.985)
    pallas_call x1, Pallas kernels: 18.1 us -> 17.9 us  [body(): pl.pallas_call(functools.partial(kernel, count, line, plane), out_shape=(...]
where the time goes in v4:
time: 20.1 us; the launch traced here: 20 us
  Pallas kernels  18.7 us (93%)
  between operations  1.29 us (6%)
    pallas_call x1, Pallas kernels, body(): pl.pallas_call(functools.partial(kernel, count, line, plane), out_shape=(...  17.9 us
    pallas_call x1, Pallas kernels, body(): pl.pallas_call(functools.partial(finish, line, plane), out_shape=(jax.Sha...  0.81 us

profile of v4, /device:TPU:0, one launch (start us, length us, event | category | flops | bytes accessed | tf_op | source)
XLA Modules:
  0.0 20.0 jit_solution(527667080014889202)
XLA Ops:
  1.3 17.9 %exchange.1 = (f32[4,4,2,5,8,128]{5,4,3,2,1,0:T(8,128)S(1)}, f32[4,4,2,5,8,128]{5,4,3,2,1,0:T(8,128)S(1)}, f32[32,128]{1,0:T(8,128)S(1)}, f32[5,8,128]{2,1,0:T(8...) custom-call(f32[4,4,2,5,8,128]{5,4,3,2,1,0:T(8,128)} %bitcast.8, ...), custom_call_target="tpu_custom_call" | custom-call | tf_op jit(solution)/shard_map/exchange/pallas_call | solution.py:400
  19.1 0.8 %finish.1 = (bf16[4,4,2,5,8,128]{5,4,3,2,1,0:T(8,128)(2,1)}, f32[5,8,128]{2,1,0:T(8,128)}, f32[5,8,128]{2,1,0:T(8,128)}, f32[5,8,128]{2,1,0:T(8,128)}) custom-call(f32[4,4,2,5,8,128]{5,4,3,2,1,0:T(8,128)S(1)} %get-tuple-element.15.weights, f32[4,4,2,5,8,128]{5,4,3,2,1,0:T(8,128)S(1)} %get-tuple-element.16.updates, f32[32,128]{1,0:T(8,128)S(1)} %get-tuple-element.17.ratios, ...), custom_call_target="tpu_custom_call" | custom-call | tf_op jit(solution)/shard_map/finish/pallas_call | solution.py:442

commit v5 on v4

--- a/solution.py
+++ b/solution.py
@@ -367,8 +367,7 @@
     def layer_copy(j):
         return pltpu.make_async_copy(rounded.at[j], weights_out.at[j], sem.at[3 + j])
 
-    @pl.loop(0, line)
-    def _(j):
+    for j in range(line):
         for at in range(plane):
             for side in range(2):
                 scale = ratios[pl.ds((j * plane + at) * 2 + side, 1), :]

time: 20.1 us -> 20.1 us (level)
  no operation moved by 1% of the time
where the time goes in v5:
time: 20.1 us; the launch traced here: 19.9 us
  Pallas kernels  18.7 us (93%)
  between operations  1.29 us (6%)
    pallas_call x1, Pallas kernels, body(): pl.pallas_call(functools.partial(kernel, count, line, plane), out_shape=(...  17.9 us
    pallas_call x1, Pallas kernels, body(): pl.pallas_call(functools.partial(finish, line, plane), out_shape=(jax.Sha...  0.81 us

profile of v5, /device:TPU:0, one launch (start us, length us, event | category | flops | bytes accessed | tf_op | source)
XLA Modules:
  0.0 19.9 jit_solution(15185283281760532942)
XLA Ops:
  1.3 17.9 %exchange.1 = (f32[4,4,2,5,8,128]{5,4,3,2,1,0:T(8,128)S(1)}, f32[4,4,2,5,8,128]{5,4,3,2,1,0:T(8,128)S(1)}, f32[32,128]{1,0:T(8,128)S(1)}, f32[5,8,128]{2,1,0:T(8...) custom-call(f32[4,4,2,5,8,128]{5,4,3,2,1,0:T(8,128)} %bitcast.8, ...), custom_call_target="tpu_custom_call" | custom-call | tf_op jit(solution)/shard_map/exchange/pallas_call | solution.py:399
  19.1 0.8 %finish.1 = (bf16[4,4,2,5,8,128]{5,4,3,2,1,0:T(8,128)(2,1)}, f32[5,8,128]{2,1,0:T(8,128)}, f32[5,8,128]{2,1,0:T(8,128)}, f32[5,8,128]{2,1,0:T(8,128)}) custom-call(f32[4,4,2,5,8,128]{5,4,3,2,1,0:T(8,128)S(1)} %get-tuple-element.15.weights, f32[4,4,2,5,8,128]{5,4,3,2,1,0:T(8,128)S(1)} %get-tuple-element.16.updates, f32[32,128]{1,0:T(8,128)S(1)} %get-tuple-element.17.ratios, ...), custom_call_target="tpu_custom_call" | custom-call | tf_op jit(solution)/shard_map/finish/pallas_call | solution.py:441
